TPU v7x, 32 devices: a whole 2x2x4 slice. The times are simulated.
32 devices in a mesh: dp: 16 (over z, y, x), mp: 2 (over core).
Axes of the slice: x: 2, y: 2, z: 4, core: 2. Of those that a mesh axis runs over, the one named last changes fastest.
Arguments:
- image_vectors_raw: bfloat16 [6144, 1152], P('dp', 'mp'), may hold values from -0.1796875 to 0.1796875
- text_vectors_raw: bfloat16 [6144, 1152], P('dp', 'mp'), may hold values from -0.1796875 to 0.1796875
- log_logit_scale: float32 [], replicated, may hold values from 0 to 1.5
- bias: float32 [], replicated, may hold values from -3 to -1
- loss_upstream_gradient: float32 [], replicated, may hold values from 0.5 to 2
Outputs:
- image_grad: float32 [6144, 1152], P('dp', 'mp')
- text_grad: float32 [6144, 1152], P('dp', 'mp')
All inputs are finite; a program needn't handle non-finite values.
Results may differ from a plain program's by a relative error of at most 0.0039.
Values may be sent and summed in bfloat16 or wider, within the bound.
A program may use at most 64 MiB of HBM per device.

v0:
```python
import functools

import jax
import jax.numpy as jnp
from jax import lax
from jax.experimental import pallas as pl
from jax.experimental.pallas import tpu as pltpu
from jax.sharding import PartitionSpec as P

MESH = pl.DeviceIdType.MESH
F32 = jnp.float32
BF16 = jnp.bfloat16
IMAGE, TEXT = 0, 1
VMEM_LIMIT = 60 << 20


def kernel(
    blocks, parts, chunks,
    image_ref, text_ref, log_scale_ref, bias_ref, upstream_ref,
    image_out, text_out,
    raw, own_unit, own_rows, own_inverse, sums, inner,
    scalars, scalar_sem, load_sem, far_send, far_recv, near_send, near_recv,
    own_send, own_recv, share_send, share_recv,
):
    width, rows = image_ref.shape
    size = rows // chunks
    steps = 2 * chunks
    me = lax.axis_index("dp")
    part = lax.axis_index("mp")
    parity = lax.rem(me, 2)
    near = me + 1 - 2 * parity

    def load(ref, side, index):
        return pltpu.make_async_copy(
            ref.at[:, pl.ds(index * size, size)], raw.at[0, side, 0, index], load_sem.at[side, index])

    for index in range(chunks):
        load(image_ref, IMAGE, index).start()
        load(text_ref, TEXT, index).start()
    constants = [
        pltpu.make_async_copy(ref, scalars.at[place], scalar_sem.at[place])
        for place, ref in enumerate((log_scale_ref, bias_ref, upstream_ref))
    ]
    for constant in constants:
        constant.start()

    def side_of(step):
        return jnp.where(step < chunks, parity, 1 - parity)

    def piece(k, side, slot, step):
        return raw.at[k, side, slot, lax.rem(step, chunks)]

    def far_copy(step):
        side = side_of(step)
        target = lax.rem(me + blocks - 2 + 4 * side, blocks)
        return pltpu.make_async_remote_copy(
            src_ref=piece(0, side, 0, step), dst_ref=piece(2, side, 0, step),
            send_sem=far_send.at[step], recv_sem=far_recv.at[step],
            device_id={"dp": target}, device_id_type=MESH)

    def near_copy(step, k):
        side = 1 - side_of(step)
        return pltpu.make_async_remote_copy(
            src_ref=piece(k, side, 0, step), dst_ref=piece(1, side, 0, step),
            send_sem=near_send.at[step], recv_sem=near_recv.at[step],
            device_id={"dp": near}, device_id_type=MESH)

    def own_copy(side, offset):
        return pltpu.make_async_remote_copy(
            src_ref=raw.at[0, side, 0], dst_ref=raw.at[0, side, parts - offset],
            send_sem=own_send.at[side, offset], recv_sem=own_recv.at[side, parts - offset],
            device_id={"mp": lax.rem(part + offset, parts)}, device_id_type=MESH)

    def share_copy(k, step, offset):
        side = side_of(step)
        return pltpu.make_async_remote_copy(
            src_ref=piece(k, side, 0, step), dst_ref=piece(k, side, parts - offset, step),
            send_sem=share_send.at[k - 1, step, offset], recv_sem=share_recv.at[k - 1, step, parts - offset],
            device_id={"mp": lax.rem(part + offset, parts)}, device_id_type=MESH)

    barrier = pltpu.get_barrier_semaphore()
    pl.semaphore_signal(barrier, inc=1, device_id={"dp": near}, device_id_type=MESH)
    pl.semaphore_signal(barrier, inc=1, device_id={"dp": lax.rem(me + 2, blocks)}, device_id_type=MESH)
    pl.semaphore_signal(barrier, inc=1, device_id={"dp": lax.rem(me + blocks - 2, blocks)}, device_id_type=MESH)
    for offset in range(1, parts):
        pl.semaphore_signal(barrier, inc=1, device_id={"mp": lax.rem(part + offset, parts)}, device_id_type=MESH)
    pl.semaphore_wait(barrier, 2 + parts)

    for step in range(chunks):
        load(image_ref, IMAGE, step).wait()
        load(text_ref, TEXT, step).wait()
        far_copy(step).start()
        near_copy(step, 0).start()
    for step in range(chunks, steps):
        far_copy(step).start()
    for side in (IMAGE, TEXT):
        for offset in range(1, parts):
            own_copy(side, offset).start()

    for constant in constants:
        constant.wait()
    scale = jnp.exp(jnp.zeros((1, 1), F32) + scalars[0, 0])
    bias = scalars[1, 0]
    weight = scale * scalars[2, 0]

    def unit_rows(k, side, index):
        wide = [raw[k, side, slot, index].astype(F32) for slot in range(parts)]
        square = sum(jnp.sum(w * w, axis=0, keepdims=True) for w in wide)
        inverse = lax.rsqrt(square + 1e-06)
        return [(w * inverse).astype(BF16) for w in wide], inverse

    def pair_terms(units, side, diagonal):
        other = 1 - side
        total = None
        for slot in range(parts):
            term = jnp.dot(own_rows[other, slot], units[slot], preferred_element_type=F32)
            total = term if total is None else total + term
        scores = scale * total + bias
        if diagonal:
            shape = total.shape
            matching = lax.broadcasted_iota(jnp.int32, shape, 0) == lax.broadcasted_iota(jnp.int32, shape, 1)
            sign = jnp.where(matching, 1.0, -1.0).astype(F32)
            factor = -weight * sign * jax.nn.sigmoid(-sign * scores)
        else:
            factor = weight * jax.nn.sigmoid(scores)
        factor = factor.astype(BF16)
        gradient = lax.dot_general(
            units[0], factor, (((1,), (1,)), ((), ())), preferred_element_type=F32)
        product = factor.astype(F32) * total
        product = sum(product[:, at:at + size] for at in range(0, product.shape[1], size))
        if diagonal:
            sums[other] = gradient
            inner[other] = product
        else:
            sums[other] += gradient
            inner[other] += product

    for side in (IMAGE, TEXT):
        for slot in range(1, parts):
            own_copy(side, parts - slot).wait_recv()

    def own_norm(index, carry):
        side, place = index // chunks, lax.rem(index, chunks)
        units, inverse = unit_rows(0, side, place)
        for slot in range(parts):
            own_unit[side, slot, place] = units[slot]
            own_rows[side, slot, pl.ds(pl.multiple_of(place * size, size), size), :] = units[slot].T
        own_inverse[side, place] = inverse
        return carry

    lax.fori_loop(0, steps, own_norm, 0)

    def own_pairs(side, carry):
        pair_terms(
            [jnp.concatenate([own_unit[side, slot, place] for place in range(chunks)], axis=1)
             for slot in range(parts)], side, True)
        return carry

    lax.fori_loop(0, 2, own_pairs, 0)

    def finish(side, out):
        for index in range(chunks):
            place = slice(index * size, (index + 1) * size)
            inverse = own_inverse[side, index]
            product = jnp.sum(inner[side, place, :].T, axis=0, keepdims=True)
            unit = raw[0, side, 0, index].astype(F32) * inverse
            out[:, place] = inverse * (sums[side, :, place] - unit * product)

    def advance(step, carry):
        @pl.when(step < steps)
        def _():
            far_copy(step).wait_recv()

            @pl.when(step < chunks)
            def _():
                near_copy(step + chunks, 2).start()

            for offset in range(1, parts):
                share_copy(2, step, offset).start()
            near_copy(step, 0).wait_recv()
            for offset in range(1, parts):
                share_copy(1, step, offset).start()

        @pl.when(step > 0)
        def _():
            past = step - 1
            side = side_of(past)
            for k in (1, 2):
                for slot in range(1, parts):
                    share_copy(k, past, parts - slot).wait_recv()
            units = [unit_rows(k, side, lax.rem(past, chunks))[0] for k in (1, 2)]
            pair_terms([jnp.concatenate(halves, axis=1) for halves in zip(*units)], side, False)

        @pl.when((step == chunks) & (parity == 0))
        def _():
            finish(TEXT, text_out)

        @pl.when((step == chunks) & (parity == 1))
        def _():
            finish(IMAGE, image_out)

        return carry

    lax.fori_loop(0, steps + 1, advance, 0)

    @pl.when(parity == 0)
    def _():
        finish(IMAGE, image_out)

    @pl.when(parity == 1)
    def _():
        finish(TEXT, text_out)

    for side in (IMAGE, TEXT):
        for offset in range(1, parts):
            own_copy(side, offset).wait_send()
    for step in range(steps):
        far_copy(step).wait_send()
        near_copy(step, 0).wait_send()
        for offset in range(1, parts):
            share_copy(1, step, offset).wait_send()
            share_copy(2, step, offset).wait_send()


def publish(image_ref, text_ref, image_out, text_out, sems):
    copies = [
        pltpu.make_async_copy(image_ref, image_out, sems.at[0]),
        pltpu.make_async_copy(text_ref, text_out, sems.at[1]),
    ]
    for copy in copies:
        copy.start()
    for copy in copies:
        copy.wait()


def solution(mesh):
    blocks, parts = mesh.shape["dp"], mesh.shape["mp"]

    def local(image, text, log_logit_scale, bias, loss_upstream_gradient):
        rows, width = image.shape
        chunks = max(rows // 128, 1)
        size = rows // chunks
        steps = 2 * chunks
        hbm = pl.BlockSpec(memory_space=pltpu.HBM)
        anywhere = pl.BlockSpec(memory_space=pl.ANY)
        whole = pl.BlockSpec(memory_space=pltpu.VMEM)
        dma = pltpu.SemaphoreType.DMA
        out = jax.ShapeDtypeStruct((width, rows), F32)
        image_grad, text_grad = pl.pallas_call(
            functools.partial(kernel, blocks, parts, chunks),
            out_shape=(pltpu.VMEM((width, rows), F32),) * 2,
            in_specs=[hbm] * 5,
            out_specs=(whole, whole),
            scratch_shapes=[
                pltpu.VMEM((3, 2, parts, chunks, width, size), BF16),
                pltpu.VMEM((2, parts, chunks, width, size), BF16),
                pltpu.VMEM((2, parts, rows, width), BF16),
                pltpu.VMEM((2, chunks, 1, size), F32),
                pltpu.VMEM((2, width, rows), F32),
                pltpu.VMEM((2, rows, size), F32),
                pltpu.SMEM((3, 1), F32), dma((3,)), dma((2, chunks)),
                dma((steps,)), dma((steps,)), dma((steps,)), dma((steps,)),
                dma((2, parts)), dma((2, parts)),
                dma((2, steps, parts)), dma((2, steps, parts)),
            ],
            compiler_params=pltpu.CompilerParams(
                collective_id=0, has_side_effects=True, vmem_limit_bytes=VMEM_LIMIT),
        )(image.T, text.T, log_logit_scale.reshape(1), bias.reshape(1), loss_upstream_gradient.reshape(1))
        image_grad, text_grad = pl.pallas_call(
            publish,
            out_shape=(out, out),
            in_specs=[anywhere, anywhere],
            out_specs=(hbm, hbm),
            scratch_shapes=[dma((2,))],
            compiler_params=pltpu.CompilerParams(vmem_limit_bytes=4 << 20),
        )(image_grad, text_grad)
        return image_grad.T, text_grad.T

    placed = (P("dp", "mp"), P("dp", "mp"), P(), P(), P())
    return jax.shard_map(
        local, mesh=mesh, in_specs=placed, out_specs=(P("dp", "mp"), P("dp", "mp")), check_vma=False
    )
```

profile of v0, /device:TPU:0, one launch (start us, length us, event | category | flops | bytes accessed | tf_op | source)
XLA Modules:
  0.0 35.4 jit_solution(13128255795838731946)
XLA Ops:
  2.6 31.6 %shard_map.68 = (f32[576,384]{1,0:T(8,128)S(1)}, f32[576,384]{1,0:T(8,128)S(1)}) custom-call(bf16[576,384]{1,0:T(8,128)(2,1)} %bitcast.10, bf16[576,384]{1,0:T(8,128)(2,1)} %bitcast.11, f32[1]{0:T(128)} %bitcast.7.log_scale_ref, f32[1]{0:T(128)} %bitcast.8.bias_ref, f32[1]{0:T(128)} %bitcast.9.upstream_ref), custom_call_target="tpu_custom_call" | custom-call | tf_op jit(solution)/shard_map/pallas_call | solution.py:249
  34.2 1.2 %shard_map.69 = (f32[576,384]{1,0:T(8,128)}, f32[576,384]{1,0:T(8,128)}) custom-call(f32[576,384]{1,0:T(8,128)S(1)} %get-tuple-element.6.image_ref, f32[576,384]{1,0:T(8,128)S(1)} %get-tuple-element.7.text_ref), custom_call_target="tpu_custom_call" | custom-call | tf_op jit(solution)/shard_map/pallas_call | solution.py:269
where the time goes:
time: 35.8 us; the launch traced here: 35.4 us
  Pallas kernels  32.8 us (92%)
  between operations  2.57 us (7%)
    pallas_call x1, Pallas kernels, local(): pl.pallas_call(functools.partial(kernel, blocks, parts, chunks), out_shap...  31.6 us
    pallas_call x1, Pallas kernels, local(): pl.pallas_call(publish, out_shape=(out, out), in_specs=[anywhere, anywher...  1.22 us

commit v1 on v0

--- a/solution.py
+++ b/solution.py
@@ -18,8 +18,8 @@
     blocks, parts, chunks,
     image_ref, text_ref, log_scale_ref, bias_ref, upstream_ref,
     image_out, text_out,
-    raw, own_unit, own_rows, own_inverse, sums, inner,
-    scalars, scalar_sem, load_sem, far_send, far_recv, near_send, near_recv,
+    raw, relay, own_unit, own_rows, own_inverse, sums, inner,
+    scalars, scalar_sem, load_sem, far_send, far_recv, near_send, near_recv, leg_send, leg_recv,
     own_send, own_recv, share_send, share_recv,
 ):
     width, rows = image_ref.shape
@@ -29,6 +29,12 @@
     part = lax.axis_index("mp")
     parity = lax.rem(me, 2)
     near = me + 1 - 2 * parity
+    late = 1 - parity
+    relayed = parity != lax.rem(me // 2, 2)
+    direct = jnp.logical_not(relayed)
+
+    def shifted(by):
+        return lax.rem(me + blocks + by, blocks)
 
     def load(ref, side, index):
         return pltpu.make_async_copy(
@@ -52,11 +58,22 @@
 
     def far_copy(step):
         side = side_of(step)
-        target = lax.rem(me + blocks - 2 + 4 * side, blocks)
         return pltpu.make_async_remote_copy(
             src_ref=piece(0, side, 0, step), dst_ref=piece(2, side, 0, step),
             send_sem=far_send.at[step], recv_sem=far_recv.at[step],
-            device_id={"dp": target}, device_id_type=MESH)
+            device_id={"dp": shifted(4 * side - 2)}, device_id_type=MESH)
+
+    def leg_copy(index):
+        return pltpu.make_async_remote_copy(
+            src_ref=raw.at[0, late, 0, index], dst_ref=relay.at[index],
+            send_sem=leg_send.at[index], recv_sem=leg_recv.at[index],
+            device_id={"dp": shifted(8 * late - 4)}, device_id_type=MESH)
+
+    def relay_copy(index):
+        return pltpu.make_async_remote_copy(
+            src_ref=relay.at[index], dst_ref=raw.at[2, late, 0, index],
+            send_sem=far_send.at[chunks + index], recv_sem=far_recv.at[chunks + index],
+            device_id={"dp": shifted(2 - 4 * late)}, device_id_type=MESH)
 
     def near_copy(step, k):
         side = 1 - side_of(step)
@@ -79,9 +96,21 @@
             device_id={"mp": lax.rem(part + offset, parts)}, device_id_type=MESH)
 
     barrier = pltpu.get_barrier_semaphore()
-    pl.semaphore_signal(barrier, inc=1, device_id={"dp": near}, device_id_type=MESH)
-    pl.semaphore_signal(barrier, inc=1, device_id={"dp": lax.rem(me + 2, blocks)}, device_id_type=MESH)
-    pl.semaphore_signal(barrier, inc=1, device_id={"dp": lax.rem(me + blocks - 2, blocks)}, device_id_type=MESH)
+
+    def greet(target):
+        pl.semaphore_signal(barrier, inc=1, device_id={"dp": target}, device_id_type=MESH)
+
+    @pl.when(relayed)
+    def _():
+        greet(shifted(2))
+        greet(shifted(-2))
+        greet(shifted(4 - 8 * late))
+
+    @pl.when(direct)
+    def _():
+        greet(shifted(2 - 4 * parity))
+
+    greet(near)
     for offset in range(1, parts):
         pl.semaphore_signal(barrier, inc=1, device_id={"mp": lax.rem(part + offset, parts)}, device_id_type=MESH)
     pl.semaphore_wait(barrier, 2 + parts)
@@ -91,8 +120,17 @@
         load(text_ref, TEXT, step).wait()
         far_copy(step).start()
         near_copy(step, 0).start()
-    for step in range(chunks, steps):
-        far_copy(step).start()
+
+    @pl.when(relayed)
+    def _():
+        for index in range(chunks):
+            leg_copy(index).start()
+
+    @pl.when(direct)
+    def _():
+        for step in range(chunks, steps):
+            far_copy(step).start()
+
     for side in (IMAGE, TEXT):
         for offset in range(1, parts):
             own_copy(side, offset).start()
@@ -175,6 +213,11 @@
             def _():
                 near_copy(step + chunks, 2).start()
 
+            @pl.when((step < chunks) & relayed)
+            def _():
+                leg_copy(step).wait_recv()
+                relay_copy(step).start()
+
             for offset in range(1, parts):
                 share_copy(2, step, offset).start()
             near_copy(step, 0).wait_recv()
@@ -214,8 +257,21 @@
     for side in (IMAGE, TEXT):
         for offset in range(1, parts):
             own_copy(side, offset).wait_send()
+
+    @pl.when(relayed)
+    def _():
+        for index in range(chunks):
+            leg_copy(index).wait_send()
+            relay_copy(index).wait_send()
+
+    @pl.when(direct)
+    def _():
+        for step in range(chunks, steps):
+            far_copy(step).wait_send()
+
     for step in range(steps):
-        far_copy(step).wait_send()
+        if step < chunks:
+            far_copy(step).wait_send()
         near_copy(step, 0).wait_send()
         for offset in range(1, parts):
             share_copy(1, step, offset).wait_send()
@@ -253,6 +309,7 @@
             out_specs=(whole, whole),
             scratch_shapes=[
                 pltpu.VMEM((3, 2, parts, chunks, width, size), BF16),
+                pltpu.VMEM((chunks, width, size), BF16),
                 pltpu.VMEM((2, parts, chunks, width, size), BF16),
                 pltpu.VMEM((2, parts, rows, width), BF16),
                 pltpu.VMEM((2, chunks, 1, size), F32),
@@ -260,6 +317,7 @@
                 pltpu.VMEM((2, rows, size), F32),
                 pltpu.SMEM((3, 1), F32), dma((3,)), dma((2, chunks)),
                 dma((steps,)), dma((steps,)), dma((steps,)), dma((steps,)),
+                dma((chunks,)), dma((chunks,)),
                 dma((2, parts)), dma((2, parts)),
                 dma((2, steps, parts)), dma((2, steps, parts)),
             ],

time: 35.8 us -> 33.5 us (0.936)
  Pallas kernels: 32.8 us -> 30.8 us
    pallas_call x1, Pallas kernels: 31.6 us -> 29.6 us  [local(): pl.pallas_call(functools.partial(kernel, blocks, parts, chunks), out_shap...]
where the time goes in v1:
time: 33.5 us; the launch traced here: 33.4 us
  Pallas kernels  30.8 us (92%)
  between operations  2.57 us (8%)
    pallas_call x1, Pallas kernels, local(): pl.pallas_call(functools.partial(kernel, blocks, parts, chunks), out_shap...  29.6 us
    pallas_call x1, Pallas kernels, local(): pl.pallas_call(publish, out_shape=(out, out), in_specs=[anywhere, anywher...  1.22 us

profile of v1, /device:TPU:0, one launch (start us, length us, event | category | flops | bytes accessed | tf_op | source)
XLA Modules:
  0.0 33.4 jit_solution(15692691540806059547)
XLA Ops:
  2.6 29.6 %shard_map.68 = (f32[576,384]{1,0:T(8,128)S(1)}, f32[576,384]{1,0:T(8,128)S(1)}) custom-call(bf16[576,384]{1,0:T(8,128)(2,1)} %bitcast.10, bf16[576,384]{1,0:T(8,128)(2,1)} %bitcast.11, f32[1]{0:T(128)} %bitcast.7.log_scale_ref, f32[1]{0:T(128)} %bitcast.8.bias_ref, f32[1]{0:T(128)} %bitcast.9.upstream_ref), custom_call_target="tpu_custom_call" | custom-call | tf_op jit(solution)/shard_map/pallas_call | solution.py:305
  32.2 1.2 %shard_map.69 = (f32[576,384]{1,0:T(8,128)}, f32[576,384]{1,0:T(8,128)}) custom-call(f32[576,384]{1,0:T(8,128)S(1)} %get-tuple-element.6.image_ref, f32[576,384]{1,0:T(8,128)S(1)} %get-tuple-element.7.text_ref), custom_call_target="tpu_custom_call" | custom-call | tf_op jit(solution)/shard_map/pallas_call | solution.py:327

commit v2 on v1

--- a/solution.py
+++ b/solution.py
@@ -16,10 +16,10 @@
 
 def kernel(
     blocks, parts, chunks,
-    image_ref, text_ref, log_scale_ref, bias_ref, upstream_ref,
+    image_ref, text_ref, constant_ref,
     image_out, text_out,
-    raw, relay, own_unit, own_rows, own_inverse, sums, inner,
-    scalars, scalar_sem, load_sem, far_send, far_recv, near_send, near_recv, leg_send, leg_recv,
+    raw, relay, own_unit, own_rows, own_inverse, sums, inner, constants,
+    load_sem, constant_send, constant_recv, far_send, far_recv, near_send, near_recv, leg_send, leg_recv,
     own_send, own_recv, share_send, share_recv,
 ):
     width, rows = image_ref.shape
@@ -32,23 +32,33 @@
     late = 1 - parity
     relayed = parity != lax.rem(me // 2, 2)
     direct = jnp.logical_not(relayed)
+    members = 2 * parts
+    member = parity * parts + part
 
     def shifted(by):
         return lax.rem(me + blocks + by, blocks)
 
     def load(ref, side, index):
         return pltpu.make_async_copy(
-            ref.at[:, pl.ds(index * size, size)], raw.at[0, side, 0, index], load_sem.at[side, index])
+            ref.at[:, pl.ds(index * size, size)], raw.at[0, side, 0, index], load_sem)
 
     for index in range(chunks):
         load(image_ref, IMAGE, index).start()
         load(text_ref, TEXT, index).start()
-    constants = [
-        pltpu.make_async_copy(ref, scalars.at[place], scalar_sem.at[place])
-        for place, ref in enumerate((log_scale_ref, bias_ref, upstream_ref))
-    ]
-    for constant in constants:
-        constant.start()
+    constants[member] = constant_ref[...]
+
+    def settle(ref, sem):
+        pltpu.make_async_copy(ref, ref, sem).wait()
+
+    def mate(offset):
+        other = lax.rem(member + offset, members)
+        return {"dp": me - parity + other // parts, "mp": lax.rem(other, parts)}
+
+    def constant_copy(offset):
+        return pltpu.make_async_remote_copy(
+            src_ref=constant_ref, dst_ref=constants.at[member],
+            send_sem=constant_send, recv_sem=constant_recv,
+            device_id=mate(offset), device_id_type=MESH)
 
     def side_of(step):
         return jnp.where(step < chunks, parity, 1 - parity)
@@ -60,39 +70,39 @@
         side = side_of(step)
         return pltpu.make_async_remote_copy(
             src_ref=piece(0, side, 0, step), dst_ref=piece(2, side, 0, step),
-            send_sem=far_send.at[step], recv_sem=far_recv.at[step],
+            send_sem=far_send, recv_sem=far_recv.at[step],
             device_id={"dp": shifted(4 * side - 2)}, device_id_type=MESH)
 
     def leg_copy(index):
         return pltpu.make_async_remote_copy(
             src_ref=raw.at[0, late, 0, index], dst_ref=relay.at[index],
-            send_sem=leg_send.at[index], recv_sem=leg_recv.at[index],
+            send_sem=leg_send, recv_sem=leg_recv.at[index],
             device_id={"dp": shifted(8 * late - 4)}, device_id_type=MESH)
 
     def relay_copy(index):
         return pltpu.make_async_remote_copy(
             src_ref=relay.at[index], dst_ref=raw.at[2, late, 0, index],
-            send_sem=far_send.at[chunks + index], recv_sem=far_recv.at[chunks + index],
+            send_sem=far_send, recv_sem=far_recv.at[chunks + index],
             device_id={"dp": shifted(2 - 4 * late)}, device_id_type=MESH)
 
     def near_copy(step, k):
         side = 1 - side_of(step)
         return pltpu.make_async_remote_copy(
             src_ref=piece(k, side, 0, step), dst_ref=piece(1, side, 0, step),
-            send_sem=near_send.at[step], recv_sem=near_recv.at[step],
+            send_sem=near_send, recv_sem=near_recv.at[step],
             device_id={"dp": near}, device_id_type=MESH)
 
     def own_copy(side, offset):
         return pltpu.make_async_remote_copy(
             src_ref=raw.at[0, side, 0], dst_ref=raw.at[0, side, parts - offset],
-            send_sem=own_send.at[side, offset], recv_sem=own_recv.at[side, parts - offset],
+            send_sem=own_send.at[offset - 1], recv_sem=own_recv.at[parts - offset - 1],
             device_id={"mp": lax.rem(part + offset, parts)}, device_id_type=MESH)
 
     def share_copy(k, step, offset):
         side = side_of(step)
         return pltpu.make_async_remote_copy(
             src_ref=piece(k, side, 0, step), dst_ref=piece(k, side, parts - offset, step),
-            send_sem=share_send.at[k - 1, step, offset], recv_sem=share_recv.at[k - 1, step, parts - offset],
+            send_sem=share_send.at[offset - 1], recv_sem=share_recv.at[step, parts - offset - 1],
             device_id={"mp": lax.rem(part + offset, parts)}, device_id_type=MESH)
 
     barrier = pltpu.get_barrier_semaphore()
@@ -110,14 +120,14 @@
     def _():
         greet(shifted(2 - 4 * parity))
 
-    greet(near)
-    for offset in range(1, parts):
-        pl.semaphore_signal(barrier, inc=1, device_id={"mp": lax.rem(part + offset, parts)}, device_id_type=MESH)
-    pl.semaphore_wait(barrier, 2 + parts)
-
+    for offset in range(1, members):
+        pl.semaphore_signal(barrier, inc=1, device_id=mate(offset), device_id_type=MESH)
+    settle(raw.at[0, :, 0], load_sem)
+    pl.semaphore_wait(barrier, 1 + members)
+
+    for offset in range(1, members):
+        constant_copy(offset).start()
     for step in range(chunks):
-        load(image_ref, IMAGE, step).wait()
-        load(text_ref, TEXT, step).wait()
         far_copy(step).start()
         near_copy(step, 0).start()
 
@@ -134,12 +144,6 @@
     for side in (IMAGE, TEXT):
         for offset in range(1, parts):
             own_copy(side, offset).start()
-
-    for constant in constants:
-        constant.wait()
-    scale = jnp.exp(jnp.zeros((1, 1), F32) + scalars[0, 0])
-    bias = scalars[1, 0]
-    weight = scale * scalars[2, 0]
 
     def unit_rows(k, side, index):
         wide = [raw[k, side, slot, index].astype(F32) for slot in range(parts)]
@@ -149,6 +153,9 @@
 
     def pair_terms(units, side, diagonal):
         other = 1 - side
+        scale = jnp.exp(constants[0, :, 0:1])
+        bias = constants[1, :, 0:1]
+        weight = scale * constants[2, :, 0:1]
         total = None
         for slot in range(parts):
             term = jnp.dot(own_rows[other, slot], units[slot], preferred_element_type=F32)
@@ -173,9 +180,8 @@
             sums[other] += gradient
             inner[other] += product
 
-    for side in (IMAGE, TEXT):
-        for slot in range(1, parts):
-            own_copy(side, parts - slot).wait_recv()
+    for slot in range(1, parts):
+        settle(raw.at[0, :, slot], own_recv.at[slot - 1])
 
     def own_norm(index, carry):
         side, place = index // chunks, lax.rem(index, chunks)
@@ -187,6 +193,7 @@
         return carry
 
     lax.fori_loop(0, steps, own_norm, 0)
+    settle(constants.at[pl.ds(1, members - 1)], constant_recv)
 
     def own_pairs(side, carry):
         pair_terms(
@@ -228,9 +235,8 @@
         def _():
             past = step - 1
             side = side_of(past)
-            for k in (1, 2):
-                for slot in range(1, parts):
-                    share_copy(k, past, parts - slot).wait_recv()
+            for slot in range(1, parts):
+                settle(raw.at[pl.ds(1, 2), side, slot, lax.rem(past, chunks)], share_recv.at[past, slot - 1])
             units = [unit_rows(k, side, lax.rem(past, chunks))[0] for k in (1, 2)]
             pair_terms([jnp.concatenate(halves, axis=1) for halves in zip(*units)], side, False)
 
@@ -254,28 +260,20 @@
     def _():
         finish(TEXT, text_out)
 
-    for side in (IMAGE, TEXT):
-        for offset in range(1, parts):
-            own_copy(side, offset).wait_send()
-
     @pl.when(relayed)
     def _():
-        for index in range(chunks):
-            leg_copy(index).wait_send()
-            relay_copy(index).wait_send()
-
-    @pl.when(direct)
-    def _():
-        for step in range(chunks, steps):
-            far_copy(step).wait_send()
-
-    for step in range(steps):
-        if step < chunks:
-            far_copy(step).wait_send()
-        near_copy(step, 0).wait_send()
-        for offset in range(1, parts):
-            share_copy(1, step, offset).wait_send()
-            share_copy(2, step, offset).wait_send()
+        settle(relay, leg_send)
+
+    settle(raw.at[0, :, 0], far_send)
+    settle(raw.at[0, :, 0], near_send)
+    settle(constants.at[pl.ds(1, members - 1)], constant_send)
+    for offset in range(1, parts):
+        settle(raw.at[0, :, 0], own_send.at[offset - 1])
+        settle(raw.at[pl.ds(0, 2), :, 0], share_send.at[offset - 1])
+
+
+def spread(value_ref, row_ref):
+    row_ref[...] = jnp.full(row_ref.shape, value_ref[0])
 
 
 def publish(image_ref, text_ref, image_out, text_out, sems):
@@ -302,10 +300,26 @@
         whole = pl.BlockSpec(memory_space=pltpu.VMEM)
         dma = pltpu.SemaphoreType.DMA
         out = jax.ShapeDtypeStruct((width, rows), F32)
+        member = lax.rem(lax.axis_index("dp"), 2) * parts + lax.axis_index("mp")
+
+        def pick(place):
+            def branch(*values):
+                return pl.pallas_call(
+                    spread,
+                    out_shape=pltpu.VMEM((1, 128), F32),
+                    in_specs=[pl.BlockSpec(memory_space=pltpu.SMEM)],
+                    out_specs=whole,
+                    name=f"constant_{place}",
+                    compiler_params=pltpu.CompilerParams(vmem_limit_bytes=1 << 20),
+                )(values[place].reshape(1))
+            return branch
+
+        constant = lax.switch(
+            lax.rem(member, 3), [pick(place) for place in range(3)], log_logit_scale, bias, loss_upstream_gradient)
         image_grad, text_grad = pl.pallas_call(
             functools.partial(kernel, blocks, parts, chunks),
             out_shape=(pltpu.VMEM((width, rows), F32),) * 2,
-            in_specs=[hbm] * 5,
+            in_specs=[hbm, hbm, whole],
             out_specs=(whole, whole),
             scratch_shapes=[
                 pltpu.VMEM((3, 2, parts, chunks, width, size), BF16),
@@ -315,15 +329,14 @@
                 pltpu.VMEM((2, chunks, 1, size), F32),
                 pltpu.VMEM((2, width, rows), F32),
                 pltpu.VMEM((2, rows, size), F32),
-                pltpu.SMEM((3, 1), F32), dma((3,)), dma((2, chunks)),
-                dma((steps,)), dma((steps,)), dma((steps,)), dma((steps,)),
-                dma((chunks,)), dma((chunks,)),
-                dma((2, parts)), dma((2, parts)),
-                dma((2, steps, parts)), dma((2, steps, parts)),
+                pltpu.VMEM((2 * parts, 1, 128), F32),
+                dma, dma, dma, dma, dma((steps,)), dma, dma((steps,)), dma, dma((chunks,)),
+                dma((parts - 1,)), dma((parts - 1,)),
+                dma((parts - 1,)), dma((steps, parts - 1)),
             ],
             compiler_params=pltpu.CompilerParams(
                 collective_id=0, has_side_effects=True, vmem_limit_bytes=VMEM_LIMIT),
-        )(image.T, text.T, log_logit_scale.reshape(1), bias.reshape(1), loss_upstream_gradient.reshape(1))
+        )(image.T, text.T, constant)
         image_grad, text_grad = pl.pallas_call(
             publish,
             out_shape=(out, out),

time: 33.5 us -> 31.7 us (0.946)
  between operations: 2.57 us -> 0.66 us
    pallas_call x0 -> x1, Pallas kernels: none -> 0.65 us  [branch(): pl.pallas_call(spread, out_shape=pltpu.VMEM((1, 128), F32), in_specs=[pl....]
    pallas_call x1, Pallas kernels: 29.6 us -> 29 us  [local(): pl.pallas_call(functools.partial(kernel, blocks, parts, chunks), out_shap...]
where the time goes in v2:
time: 31.7 us; the launch traced here: 31.5 us
  Pallas kernels  30.8 us (97%)
  between operations  0.66 us (2%)
    pallas_call x1, Pallas kernels, local(): pl.pallas_call(functools.partial(kernel, blocks, parts, chunks), out_shap...  29 us
    pallas_call x1, Pallas kernels, local(): pl.pallas_call(publish, out_shape=(out, out), in_specs=[anywhere, anywher...  1.22 us
    pallas_call x1, Pallas kernels, branch(): pl.pallas_call(spread, out_shape=pltpu.VMEM((1, 128), F32), in_specs=[pl....  0.65 us

profile of v2, /device:TPU:0, one launch (start us, length us, event | category | flops | bytes accessed | tf_op | source)
XLA Modules:
  0.0 31.5 jit_solution(4164332462162582461)
XLA Ops:
  0.6 0.7 %conditional.1 = (f32[1,128]{1,0:T(1,128)S(1)}) conditional(s32[]{:T(128)} %clamp.3, (f32[]{:T(128)}) %tuple.18, (f32[]{:T(128)}) %tuple.19, (f32[]{:T(128)}) %tuple.20), branch_computations={%region_0.0_spmd, %region_1.0_spmd, %region_2.0_spmd} | conditional | bytes 8 | solution.py:317
  0.7 0.6 %constant_0.1 = f32[1,128]{1,0:T(1,128)S(1)} custom-call(f32[1]{0:T(128)} %bitcast.value_ref), custom_call_target="tpu_custom_call" | custom-call | tf_op jit(solution)/shard_map/cond/branch_0_fun/constant_0/pallas_call | solution.py:307
  1.3 29.0 %shard_map.80 = (f32[576,384]{1,0:T(8,128)S(1)}, f32[576,384]{1,0:T(8,128)S(1)}) custom-call(bf16[576,384]{1,0:T(8,128)(2,1)} %bitcast.7, bf16[576,384]{1,0:T(8,128)(2,1)} %bitcast.8, f32[1,128]{1,0:T(1,128)S(1)} %get-tuple-element.23.constant_ref), custom_call_target="tpu_custom_call" | custom-call | tf_op jit(solution)/shard_map/pallas_call | solution.py:319
  30.3 1.2 %shard_map.81 = (f32[576,384]{1,0:T(8,128)}, f32[576,384]{1,0:T(8,128)}) custom-call(f32[576,384]{1,0:T(8,128)S(1)} %get-tuple-element.13.image_ref, f32[576,384]{1,0:T(8,128)S(1)} %get-tuple-element.14.text_ref), custom_call_target="tpu_custom_call" | custom-call | tf_op jit(solution)/shard_map/pallas_call | solution.py:340

commit v3 on v2

--- a/solution.py
+++ b/solution.py
@@ -20,7 +20,7 @@
     image_out, text_out,
     raw, relay, own_unit, own_rows, own_inverse, sums, inner, constants,
     load_sem, constant_send, constant_recv, far_send, far_recv, near_send, near_recv, leg_send, leg_recv,
-    own_send, own_recv, share_send, share_recv,
+    own_send, own_recv, share_send, share_recv, token,
 ):
     width, rows = image_ref.shape
     size = rows // chunks
@@ -30,7 +30,8 @@
     parity = lax.rem(me, 2)
     near = me + 1 - 2 * parity
     late = 1 - parity
-    relayed = parity != lax.rem(me // 2, 2)
+    row = lax.rem(me // 2, 2)
+    relayed = parity != row
     direct = jnp.logical_not(relayed)
     members = 2 * parts
     member = parity * parts + part
@@ -110,31 +111,33 @@
     def greet(target):
         pl.semaphore_signal(barrier, inc=1, device_id={"dp": target}, device_id_type=MESH)
 
+    greet(shifted(2 - 4 * row))
+
     @pl.when(relayed)
     def _():
-        greet(shifted(2))
-        greet(shifted(-2))
-        greet(shifted(4 - 8 * late))
-
-    @pl.when(direct)
-    def _():
-        greet(shifted(2 - 4 * parity))
+        greet(shifted(-2 - 2 * row))
 
     for offset in range(1, members):
         pl.semaphore_signal(barrier, inc=1, device_id=mate(offset), device_id_type=MESH)
     settle(raw.at[0, :, 0], load_sem)
-    pl.semaphore_wait(barrier, 1 + members)
+    pl.semaphore_wait(barrier, row + members)
 
     for offset in range(1, members):
         constant_copy(offset).start()
+
+    def inform(target):
+        pl.semaphore_signal(token, inc=1, device_id={"dp": target}, device_id_type=MESH)
+
+    @pl.when(row == 1)
+    def _():
+        inform(shifted(4 - 2 * parity))
+
     for step in range(chunks):
-        far_copy(step).start()
+        @pl.when(parity + row > 0)
+        def _():
+            far_copy(step).start()
+
         near_copy(step, 0).start()
-
-    @pl.when(relayed)
-    def _():
-        for index in range(chunks):
-            leg_copy(index).start()
 
     @pl.when(direct)
     def _():
@@ -180,6 +183,25 @@
             sums[other] += gradient
             inner[other] += product
 
+    @pl.when((parity == 0) & (row == 1))
+    def _():
+        for index in range(chunks):
+            leg_copy(index).start()
+        pl.semaphore_wait(token, 1)
+        inform(shifted(-2))
+
+    @pl.when((parity == 0) & (row == 0))
+    def _():
+        pl.semaphore_wait(token, 1)
+        for step in range(chunks):
+            far_copy(step).start()
+
+    @pl.when((parity == 1) & (row == 0))
+    def _():
+        pl.semaphore_wait(token, 1)
+        for index in range(chunks):
+            leg_copy(index).start()
+
     for slot in range(1, parts):
         settle(raw.at[0, :, slot], own_recv.at[slot - 1])
 
@@ -332,7 +354,7 @@
                 pltpu.VMEM((2 * parts, 1, 128), F32),
                 dma, dma, dma, dma, dma((steps,)), dma, dma((steps,)), dma, dma((chunks,)),
                 dma((parts - 1,)), dma((parts - 1,)),
-                dma((parts - 1,)), dma((steps, parts - 1)),
+                dma((parts - 1,)), dma((steps, parts - 1)), pltpu.SemaphoreType.REGULAR,
             ],
             compiler_params=pltpu.CompilerParams(
                 collective_id=0, has_side_effects=True, vmem_limit_bytes=VMEM_LIMIT),

time: 31.7 us -> 30.2 us (0.953)
  Pallas kernels: 30.8 us -> 29.4 us
    pallas_call x1, Pallas kernels: 29 us -> 27.5 us  [local(): pl.pallas_call(functools.partial(kernel, blocks, parts, chunks), out_shap...]
where the time goes in v3:
time: 30.2 us; the launch traced here: 30.1 us
  Pallas kernels  29.4 us (97%)
  between operations  0.66 us (2%)
    pallas_call x1, Pallas kernels, local(): pl.pallas_call(functools.partial(kernel, blocks, parts, chunks), out_shap...  27.5 us
    pallas_call x1, Pallas kernels, local(): pl.pallas_call(publish, out_shape=(out, out), in_specs=[anywhere, anywher...  1.22 us
    pallas_call x1, Pallas kernels, branch(): pl.pallas_call(spread, out_shape=pltpu.VMEM((1, 128), F32), in_specs=[pl....  0.65 us

profile of v3, /device:TPU:0, one launch (start us, length us, event | category | flops | bytes accessed | tf_op | source)
XLA Modules:
  0.0 30.1 jit_solution(10338116345352727131)
XLA Ops:
  0.6 0.7 %conditional.1 = (f32[1,128]{1,0:T(1,128)S(1)}) conditional(s32[]{:T(128)} %clamp.3, (f32[]{:T(128)}) %tuple.18, (f32[]{:T(128)}) %tuple.19, (f32[]{:T(128)}) %tuple.20), branch_computations={%region_0.0_spmd, %region_1.0_spmd, %region_2.0_spmd} | conditional | bytes 8 | solution.py:339
  0.7 0.6 %constant_0.1 = f32[1,128]{1,0:T(1,128)S(1)} custom-call(f32[1]{0:T(128)} %bitcast.value_ref), custom_call_target="tpu_custom_call" | custom-call | tf_op jit(solution)/shard_map/cond/branch_0_fun/constant_0/pallas_call | solution.py:329
  1.3 27.5 %shard_map.80 = (f32[576,384]{1,0:T(8,128)S(1)}, f32[576,384]{1,0:T(8,128)S(1)}) custom-call(bf16[576,384]{1,0:T(8,128)(2,1)} %bitcast.7, bf16[576,384]{1,0:T(8,128)(2,1)} %bitcast.8, f32[1,128]{1,0:T(1,128)S(1)} %get-tuple-element.23.constant_ref), custom_call_target="tpu_custom_call" | custom-call | tf_op jit(solution)/shard_map/pallas_call | solution.py:341
  28.8 1.2 %shard_map.81 = (f32[576,384]{1,0:T(8,128)}, f32[576,384]{1,0:T(8,128)}) custom-call(f32[576,384]{1,0:T(8,128)S(1)} %get-tuple-element.13.image_ref, f32[576,384]{1,0:T(8,128)S(1)} %get-tuple-element.14.text_ref), custom_call_target="tpu_custom_call" | custom-call | tf_op jit(solution)/shard_map/pallas_call | solution.py:362

commit v4 on v3

--- a/solution.py
+++ b/solution.py
@@ -17,8 +17,8 @@
 def kernel(
     blocks, parts, chunks,
     image_ref, text_ref, constant_ref,
-    image_out, text_out,
-    raw, relay, own_unit, own_rows, own_inverse, sums, inner, constants,
+    early_out, unit_out, sums, inner, own_inverse,
+    raw, relay, own_unit, own_rows, constants,
     load_sem, constant_send, constant_recv, far_send, far_recv, near_send, near_recv, leg_send, leg_recv,
     own_send, own_recv, share_send, share_recv, token,
 ):
@@ -159,10 +159,7 @@
         scale = jnp.exp(constants[0, :, 0:1])
         bias = constants[1, :, 0:1]
         weight = scale * constants[2, :, 0:1]
-        total = None
-        for slot in range(parts):
-            term = jnp.dot(own_rows[other, slot], units[slot], preferred_element_type=F32)
-            total = term if total is None else total + term
+        total = jnp.dot(own_rows[other], jnp.concatenate(units, axis=0), preferred_element_type=F32)
         scores = scale * total + bias
         if diagonal:
             shape = total.shape
@@ -210,7 +207,7 @@
         units, inverse = unit_rows(0, side, place)
         for slot in range(parts):
             own_unit[side, slot, place] = units[slot]
-            own_rows[side, slot, pl.ds(pl.multiple_of(place * size, size), size), :] = units[slot].T
+        own_rows[side, pl.ds(pl.multiple_of(place * size, size), size), :] = jnp.concatenate(units, axis=0).T
         own_inverse[side, place] = inverse
         return carry
 
@@ -225,13 +222,16 @@
 
     lax.fori_loop(0, 2, own_pairs, 0)
 
-    def finish(side, out):
+    def place_of(index):
+        return slice(index * size, (index + 1) * size)
+
+    def early_finish():
         for index in range(chunks):
-            place = slice(index * size, (index + 1) * size)
-            inverse = own_inverse[side, index]
-            product = jnp.sum(inner[side, place, :].T, axis=0, keepdims=True)
-            unit = raw[0, side, 0, index].astype(F32) * inverse
-            out[:, place] = inverse * (sums[side, :, place] - unit * product)
+            place = place_of(index)
+            early_out[:, place] = finish(
+                sums[late, :, place], inner[late, place], own_inverse[late, index],
+                raw[0, late, 0, index].astype(F32) * own_inverse[late, index])
+            unit_out[:, place] = raw[0, parity, 0, index].astype(F32) * own_inverse[parity, index]
 
     def advance(step, carry):
         @pl.when(step < steps)
@@ -262,25 +262,13 @@
             units = [unit_rows(k, side, lax.rem(past, chunks))[0] for k in (1, 2)]
             pair_terms([jnp.concatenate(halves, axis=1) for halves in zip(*units)], side, False)
 
-        @pl.when((step == chunks) & (parity == 0))
-        def _():
-            finish(TEXT, text_out)
-
-        @pl.when((step == chunks) & (parity == 1))
-        def _():
-            finish(IMAGE, image_out)
+        @pl.when(step == chunks)
+        def _():
+            early_finish()
 
         return carry
 
     lax.fori_loop(0, steps + 1, advance, 0)
-
-    @pl.when(parity == 0)
-    def _():
-        finish(IMAGE, image_out)
-
-    @pl.when(parity == 1)
-    def _():
-        finish(TEXT, text_out)
 
     @pl.when(relayed)
     def _():
@@ -298,15 +286,32 @@
     row_ref[...] = jnp.full(row_ref.shape, value_ref[0])
 
 
-def publish(image_ref, text_ref, image_out, text_out, sems):
-    copies = [
-        pltpu.make_async_copy(image_ref, image_out, sems.at[0]),
-        pltpu.make_async_copy(text_ref, text_out, sems.at[1]),
-    ]
-    for copy in copies:
-        copy.start()
-    for copy in copies:
-        copy.wait()
+def finish(gradient, products, inverse, unit):
+    inner = jnp.sum(products.T, axis=0, keepdims=True)
+    return inverse * (gradient - unit * inner)
+
+
+def publish(early_ref, unit_ref, sums, inner, own_inverse, image_out, text_out, late_ref, early_sem, late_sem):
+    parity = lax.rem(lax.axis_index("dp"), 2)
+    chunks, _, size = own_inverse.shape[1:]
+
+    def emit(first, second, ref, place, sem):
+        @pl.when(parity == 0)
+        def _():
+            pltpu.make_async_copy(ref.at[:, place], first.at[:, place], sem).start()
+
+        @pl.when(parity == 1)
+        def _():
+            pltpu.make_async_copy(ref.at[:, place], second.at[:, place], sem).start()
+
+    emit(text_out, image_out, early_ref, slice(None), early_sem)
+    for index in range(chunks):
+        place = slice(index * size, (index + 1) * size)
+        late_ref[:, place] = finish(
+            sums[parity, :, place], inner[parity, place], own_inverse[parity, index], unit_ref[:, place])
+        emit(image_out, text_out, late_ref, place, late_sem)
+    pltpu.make_async_copy(early_ref, early_ref, early_sem).wait()
+    pltpu.make_async_copy(late_ref, late_ref, late_sem).wait()
 
 
 def solution(mesh):
@@ -318,7 +323,6 @@
         size = rows // chunks
         steps = 2 * chunks
         hbm = pl.BlockSpec(memory_space=pltpu.HBM)
-        anywhere = pl.BlockSpec(memory_space=pl.ANY)
         whole = pl.BlockSpec(memory_space=pltpu.VMEM)
         dma = pltpu.SemaphoreType.DMA
         out = jax.ShapeDtypeStruct((width, rows), F32)
@@ -338,19 +342,19 @@
 
         constant = lax.switch(
             lax.rem(member, 3), [pick(place) for place in range(3)], log_logit_scale, bias, loss_upstream_gradient)
-        image_grad, text_grad = pl.pallas_call(
+        results = pl.pallas_call(
             functools.partial(kernel, blocks, parts, chunks),
-            out_shape=(pltpu.VMEM((width, rows), F32),) * 2,
+            out_shape=(
+                pltpu.VMEM((width, rows), F32), pltpu.VMEM((width, rows), F32),
+                pltpu.VMEM((2, width, rows), F32), pltpu.VMEM((2, rows, size), F32),
+                pltpu.VMEM((2, chunks, 1, size), F32)),
             in_specs=[hbm, hbm, whole],
-            out_specs=(whole, whole),
+            out_specs=(whole,) * 5,
             scratch_shapes=[
                 pltpu.VMEM((3, 2, parts, chunks, width, size), BF16),
                 pltpu.VMEM((chunks, width, size), BF16),
                 pltpu.VMEM((2, parts, chunks, width, size), BF16),
-                pltpu.VMEM((2, parts, rows, width), BF16),
-                pltpu.VMEM((2, chunks, 1, size), F32),
-                pltpu.VMEM((2, width, rows), F32),
-                pltpu.VMEM((2, rows, size), F32),
+                pltpu.VMEM((2, rows, parts * width), BF16),
                 pltpu.VMEM((2 * parts, 1, 128), F32),
                 dma, dma, dma, dma, dma((steps,)), dma, dma((steps,)), dma, dma((chunks,)),
                 dma((parts - 1,)), dma((parts - 1,)),
@@ -362,11 +366,11 @@
         image_grad, text_grad = pl.pallas_call(
             publish,
             out_shape=(out, out),
-            in_specs=[anywhere, anywhere],
+            in_specs=[whole] * 5,
             out_specs=(hbm, hbm),
-            scratch_shapes=[dma((2,))],
-            compiler_params=pltpu.CompilerParams(vmem_limit_bytes=4 << 20),
-        )(image_grad, text_grad)
+            scratch_shapes=[pltpu.VMEM((width, rows), F32), dma, dma],
+            compiler_params=pltpu.CompilerParams(vmem_limit_bytes=16 << 20),
+        )(*results)
         return image_grad.T, text_grad.T
 
     placed = (P("dp", "mp"), P("dp", "mp"), P(), P(), P())

time: 30.2 us -> 29.8 us (0.987)
  Pallas kernels: 29.4 us -> 29 us
    pallas_call x1, Pallas kernels: 27.5 us -> 27.1 us  [local(): pl.pallas_call(functools.partial(kernel, blocks, parts, chunks), out_shap...]
where the time goes in v4:
time: 29.8 us; the launch traced here: 29.7 us
  Pallas kernels  29 us (97%)
  between operations  0.66 us (2%)
    pallas_call x1, Pallas kernels, local(): pl.pallas_call(functools.partial(kernel, blocks, parts, chunks), out_shap...  27.1 us
    pallas_call x1, Pallas kernels, local(): pl.pallas_call(publish, out_shape=(out, out), in_specs=[whole] * 5, out_s...  1.23 us
    pallas_call x1, Pallas kernels, branch(): pl.pallas_call(spread, out_shape=pltpu.VMEM((1, 128), F32), in_specs=[pl....  0.65 us

profile of v4, /device:TPU:0, one launch (start us, length us, event | category | flops | bytes accessed | tf_op | source)
XLA Modules:
  0.0 29.7 jit_solution(6552883618737679791)
XLA Ops:
  0.6 0.7 %conditional.1 = (f32[1,128]{1,0:T(1,128)S(1)}) conditional(s32[]{:T(128)} %clamp.3, (f32[]{:T(128)}) %tuple.18, (f32[]{:T(128)}) %tuple.19, (f32[]{:T(128)}) %tuple.20), branch_computations={%region_0.0_spmd, %region_1.0_spmd, %region_2.0_spmd} | conditional | bytes 8 | solution.py:343
  0.7 0.6 %constant_0.1 = f32[1,128]{1,0:T(1,128)S(1)} custom-call(f32[1]{0:T(128)} %bitcast.value_ref), custom_call_target="tpu_custom_call" | custom-call | tf_op jit(solution)/shard_map/cond/branch_0_fun/constant_0/pallas_call | solution.py:333
  1.3 27.1 %shard_map.80 = (f32[576,384]{1,0:T(8,128)S(1)}, f32[576,384]{1,0:T(8,128)S(1)}, f32[2,576,384]{2,1,0:T(8,128)S(1)}, f32[2,384,128]{2,1,0:T(8,128)S(1)}, f32[2,3,1,128]{3,2,1,0:T(1,128)S(1)}) custom-call(bf16[576,384]{1,0:T(8,128)(2,1)} %bitcast.7, bf16[576,384]{1,0:T(8,128)(2,1)} %bitcast.8, f32[1,128]{1,0:T(1,128)S(1)} %get-tuple-element.29.constant_ref), custom_call_target="tpu_custom_call" | custom-call | tf_op jit(solution)/shard_map/pallas_call | solution.py:345
  28.4 1.2 %shard_map.81 = (f32[576,384]{1,0:T(8,128)}, f32[576,384]{1,0:T(8,128)}) custom-call(f32[576,384]{1,0:T(8,128)S(1)} %get-tuple-element.16.early_ref, f32[576,384]{1,0:T(8,128)S(1)} %get-tuple-element.17.unit_ref, f32[2,576,384]{2,1,0:T(8,128)S(1)} %get-tuple-element.18.sums, f32[2,384,128]{2,1,0:T(8,128)S(1)} %get-tuple-element.19.inner, ...), custom_call_target="tpu_custom_call" | custom-call | tf_op jit(solution)/shard_map/pallas_call | solution.py:366

commit v5 on v4

--- a/solution.py
+++ b/solution.py
@@ -34,6 +34,8 @@
     relayed = parity != row
     direct = jnp.logical_not(relayed)
     members = 2 * parts
+    final = steps - 1
+    beside = lax.rem(part + 1, parts)
     member = parity * parts + part
 
     def shifted(by):
@@ -64,15 +66,21 @@
     def side_of(step):
         return jnp.where(step < chunks, parity, 1 - parity)
 
+    def landing(step):
+        return jnp.where(step == final, parts - 1, 0)
+
+    def lander(step):
+        return jnp.where(step == final, beside, part)
+
     def piece(k, side, slot, step):
         return raw.at[k, side, slot, lax.rem(step, chunks)]
 
     def far_copy(step):
         side = side_of(step)
         return pltpu.make_async_remote_copy(
-            src_ref=piece(0, side, 0, step), dst_ref=piece(2, side, 0, step),
+            src_ref=piece(0, side, 0, step), dst_ref=piece(2, side, landing(step), step),
             send_sem=far_send, recv_sem=far_recv.at[step],
-            device_id={"dp": shifted(4 * side - 2)}, device_id_type=MESH)
+            device_id={"dp": shifted(4 * side - 2), "mp": lander(step)}, device_id_type=MESH)
 
     def leg_copy(index):
         return pltpu.make_async_remote_copy(
@@ -82,16 +90,16 @@
 
     def relay_copy(index):
         return pltpu.make_async_remote_copy(
-            src_ref=relay.at[index], dst_ref=raw.at[2, late, 0, index],
+            src_ref=relay.at[index], dst_ref=raw.at[2, late, landing(chunks + index), index],
             send_sem=far_send, recv_sem=far_recv.at[chunks + index],
-            device_id={"dp": shifted(2 - 4 * late)}, device_id_type=MESH)
+            device_id={"dp": shifted(2 - 4 * late), "mp": lander(chunks + index)}, device_id_type=MESH)
 
     def near_copy(step, k):
         side = 1 - side_of(step)
         return pltpu.make_async_remote_copy(
-            src_ref=piece(k, side, 0, step), dst_ref=piece(1, side, 0, step),
+            src_ref=piece(k, side, 0, step), dst_ref=piece(1, side, landing(step), step),
             send_sem=near_send, recv_sem=near_recv.at[step],
-            device_id={"dp": near}, device_id_type=MESH)
+            device_id={"dp": near, "mp": lander(step)}, device_id_type=MESH)
 
     def own_copy(side, offset):
         return pltpu.make_async_remote_copy(
@@ -102,7 +110,8 @@
     def share_copy(k, step, offset):
         side = side_of(step)
         return pltpu.make_async_remote_copy(
-            src_ref=piece(k, side, 0, step), dst_ref=piece(k, side, parts - offset, step),
+            src_ref=piece(k, side, landing(step), step),
+            dst_ref=piece(k, side, parts - offset - jnp.where(step == final, 1, 0), step),
             send_sem=share_send.at[offset - 1], recv_sem=share_recv.at[step, parts - offset - 1],
             device_id={"mp": lax.rem(part + offset, parts)}, device_id_type=MESH)
 
@@ -112,6 +121,9 @@
         pl.semaphore_signal(barrier, inc=1, device_id={"dp": target}, device_id_type=MESH)
 
     greet(shifted(2 - 4 * row))
+    pl.semaphore_signal(
+        barrier, inc=1, device_id={"dp": shifted(2 - 4 * row), "mp": lax.rem(part + parts - 1, parts)},
+        device_id_type=MESH)
 
     @pl.when(relayed)
     def _():
@@ -120,7 +132,7 @@
     for offset in range(1, members):
         pl.semaphore_signal(barrier, inc=1, device_id=mate(offset), device_id_type=MESH)
     settle(raw.at[0, :, 0], load_sem)
-    pl.semaphore_wait(barrier, row + members)
+    pl.semaphore_wait(barrier, 1 + row + members)
 
     for offset in range(1, members):
         constant_copy(offset).start()

time: 29.8 us -> 29.5 us (0.990)
  Pallas kernels: 29 us -> 28.7 us
where the time goes in v5:
time: 29.5 us; the launch traced here: 29.4 us
  Pallas kernels  28.7 us (97%)
  between operations  0.66 us (2%)
    pallas_call x1, Pallas kernels, local(): pl.pallas_call(functools.partial(kernel, blocks, parts, chunks), out_shap...  26.8 us
    pallas_call x1, Pallas kernels, local(): pl.pallas_call(publish, out_shape=(out, out), in_specs=[whole] * 5, out_s...  1.23 us
    pallas_call x1, Pallas kernels, branch(): pl.pallas_call(spread, out_shape=pltpu.VMEM((1, 128), F32), in_specs=[pl....  0.65 us

profile of v5, /device:TPU:0, one launch (start us, length us, event | category | flops | bytes accessed | tf_op | source)
XLA Modules:
  0.0 29.4 jit_solution(5248166935942941168)
XLA Ops:
  0.6 0.7 %conditional.1 = (f32[1,128]{1,0:T(1,128)S(1)}) conditional(s32[]{:T(128)} %clamp.3, (f32[]{:T(128)}) %tuple.18, (f32[]{:T(128)}) %tuple.19, (f32[]{:T(128)}) %tuple.20), branch_computations={%region_0.0_spmd, %region_1.0_spmd, %region_2.0_spmd} | conditional | bytes 8 | solution.py:355
  0.7 0.6 %constant_0.1 = f32[1,128]{1,0:T(1,128)S(1)} custom-call(f32[1]{0:T(128)} %bitcast.value_ref), custom_call_target="tpu_custom_call" | custom-call | tf_op jit(solution)/shard_map/cond/branch_0_fun/constant_0/pallas_call | solution.py:345
  1.3 26.8 %shard_map.80 = (f32[576,384]{1,0:T(8,128)S(1)}, f32[576,384]{1,0:T(8,128)S(1)}, f32[2,576,384]{2,1,0:T(8,128)S(1)}, f32[2,384,128]{2,1,0:T(8,128)S(1)}, f32[2,3,1,128]{3,2,1,0:T(1,128)S(1)}) custom-call(bf16[576,384]{1,0:T(8,128)(2,1)} %bitcast.7, bf16[576,384]{1,0:T(8,128)(2,1)} %bitcast.8, f32[1,128]{1,0:T(1,128)S(1)} %get-tuple-element.29.constant_ref), custom_call_target="tpu_custom_call" | custom-call | tf_op jit(solution)/shard_map/pallas_call | solution.py:357
  28.1 1.2 %shard_map.81 = (f32[576,384]{1,0:T(8,128)}, f32[576,384]{1,0:T(8,128)}) custom-call(f32[576,384]{1,0:T(8,128)S(1)} %get-tuple-element.16.early_ref, f32[576,384]{1,0:T(8,128)S(1)} %get-tuple-element.17.unit_ref, f32[2,576,384]{2,1,0:T(8,128)S(1)} %get-tuple-element.18.sums, f32[2,384,128]{2,1,0:T(8,128)S(1)} %get-tuple-element.19.inner, ...), custom_call_target="tpu_custom_call" | custom-call | tf_op jit(solution)/shard_map/pallas_call | solution.py:378

commit v6 on v4

--- a/solution.py
+++ b/solution.py
@@ -34,6 +34,9 @@
     relayed = parity != row
     direct = jnp.logical_not(relayed)
     members = 2 * parts
+    end, final = chunks - 1, steps - 1
+    half = width // 2
+    beside = lax.rem(part + 1, parts)
     member = parity * parts + part
 
     def shifted(by):
@@ -93,6 +96,33 @@
             send_sem=near_send, recv_sem=near_recv.at[step],
             device_id={"dp": near}, device_id_type=MESH)
 
+    def end_piece(k, side, slot, cut):
+        return raw.at[k, side, slot, end, pl.ds(cut * half, half)]
+
+    def far_end(cut):
+        return pltpu.make_async_remote_copy(
+            src_ref=end_piece(0, late, 0, cut), dst_ref=end_piece(2, late, parts - 1, cut),
+            send_sem=far_send, recv_sem=far_recv.at[final + cut],
+            device_id={"dp": shifted(4 * late - 2), "mp": beside}, device_id_type=MESH)
+
+    def relay_end(cut):
+        return pltpu.make_async_remote_copy(
+            src_ref=relay.at[end, pl.ds(cut * half, half)], dst_ref=end_piece(2, late, parts - 1, cut),
+            send_sem=far_send, recv_sem=far_recv.at[final + cut],
+            device_id={"dp": shifted(2 - 4 * late), "mp": beside}, device_id_type=MESH)
+
+    def near_end(cut):
+        return pltpu.make_async_remote_copy(
+            src_ref=end_piece(2, parity, 0, cut), dst_ref=end_piece(1, parity, parts - 1, cut),
+            send_sem=near_send, recv_sem=near_recv.at[final + cut],
+            device_id={"dp": near, "mp": beside}, device_id_type=MESH)
+
+    def share_end(k, cut, offset):
+        return pltpu.make_async_remote_copy(
+            src_ref=end_piece(k, late, parts - 1, cut), dst_ref=end_piece(k, late, parts - 1 - offset, cut),
+            send_sem=share_send.at[offset - 1], recv_sem=share_recv.at[final, parts - offset - 1],
+            device_id={"mp": lax.rem(part + offset, parts)}, device_id_type=MESH)
+
     def own_copy(side, offset):
         return pltpu.make_async_remote_copy(
             src_ref=raw.at[0, side, 0], dst_ref=raw.at[0, side, parts - offset],
@@ -112,6 +142,9 @@
         pl.semaphore_signal(barrier, inc=1, device_id={"dp": target}, device_id_type=MESH)
 
     greet(shifted(2 - 4 * row))
+    pl.semaphore_signal(
+        barrier, inc=1, device_id={"dp": shifted(2 - 4 * row), "mp": lax.rem(part + parts - 1, parts)},
+        device_id_type=MESH)
 
     @pl.when(relayed)
     def _():
@@ -120,7 +153,7 @@
     for offset in range(1, members):
         pl.semaphore_signal(barrier, inc=1, device_id=mate(offset), device_id_type=MESH)
     settle(raw.at[0, :, 0], load_sem)
-    pl.semaphore_wait(barrier, row + members)
+    pl.semaphore_wait(barrier, 1 + row + members)
 
     for offset in range(1, members):
         constant_copy(offset).start()
@@ -141,8 +174,10 @@
 
     @pl.when(direct)
     def _():
-        for step in range(chunks, steps):
+        for step in range(chunks, final):
             far_copy(step).start()
+        for cut in (0, 1):
+            far_end(cut).start()
 
     for side in (IMAGE, TEXT):
         for offset in range(1, parts):
@@ -233,34 +268,65 @@
                 raw[0, late, 0, index].astype(F32) * own_inverse[late, index])
             unit_out[:, place] = raw[0, parity, 0, index].astype(F32) * own_inverse[parity, index]
 
+    def band_pairs(step):
+        side = side_of(step)
+        for slot in range(1, parts):
+            settle(raw.at[pl.ds(1, 2), side, slot, lax.rem(step, chunks)], share_recv.at[step, slot - 1])
+        units = [unit_rows(k, side, lax.rem(step, chunks))[0] for k in (1, 2)]
+        pair_terms([jnp.concatenate(halves, axis=1) for halves in zip(*units)], side, False)
+
+    def arrive(step):
+        far_copy(step).wait_recv()
+
+        @pl.when(step < end)
+        def _():
+            near_copy(step + chunks, 2).start()
+
+        @pl.when(step == end)
+        def _():
+            for cut in (0, 1):
+                near_end(cut).start()
+
+        @pl.when((step < chunks) & relayed)
+        def _():
+            leg_copy(step).wait_recv()
+
+            @pl.when(step < end)
+            def _():
+                relay_copy(step).start()
+
+            @pl.when(step == end)
+            def _():
+                for cut in (0, 1):
+                    relay_end(cut).start()
+
+        for offset in range(1, parts):
+            share_copy(2, step, offset).start()
+        near_copy(step, 0).wait_recv()
+        for offset in range(1, parts):
+            share_copy(1, step, offset).start()
+
+    def arrive_end():
+        for cut in (0, 1):
+            far_end(cut).wait_recv()
+            for offset in range(1, parts):
+                share_end(2, cut, offset).start()
+            near_end(cut).wait_recv()
+            for offset in range(1, parts):
+                share_end(1, cut, offset).start()
+
     def advance(step, carry):
-        @pl.when(step < steps)
-        def _():
-            far_copy(step).wait_recv()
-
-            @pl.when(step < chunks)
-            def _():
-                near_copy(step + chunks, 2).start()
-
-            @pl.when((step < chunks) & relayed)
-            def _():
-                leg_copy(step).wait_recv()
-                relay_copy(step).start()
-
-            for offset in range(1, parts):
-                share_copy(2, step, offset).start()
-            near_copy(step, 0).wait_recv()
-            for offset in range(1, parts):
-                share_copy(1, step, offset).start()
+        @pl.when(step < final)
+        def _():
+            arrive(step)
+
+        @pl.when(step == final)
+        def _():
+            arrive_end()
 
         @pl.when(step > 0)
         def _():
-            past = step - 1
-            side = side_of(past)
-            for slot in range(1, parts):
-                settle(raw.at[pl.ds(1, 2), side, slot, lax.rem(past, chunks)], share_recv.at[past, slot - 1])
-            units = [unit_rows(k, side, lax.rem(past, chunks))[0] for k in (1, 2)]
-            pair_terms([jnp.concatenate(halves, axis=1) for halves in zip(*units)], side, False)
+            band_pairs(step - 1)
 
         @pl.when(step == chunks)
         def _():
@@ -356,7 +422,7 @@
                 pltpu.VMEM((2, parts, chunks, width, size), BF16),
                 pltpu.VMEM((2, rows, parts * width), BF16),
                 pltpu.VMEM((2 * parts, 1, 128), F32),
-                dma, dma, dma, dma, dma((steps,)), dma, dma((steps,)), dma, dma((chunks,)),
+                dma, dma, dma, dma, dma((steps + 1,)), dma, dma((steps + 1,)), dma, dma((chunks,)),
                 dma((parts - 1,)), dma((parts - 1,)),
                 dma((parts - 1,)), dma((steps, parts - 1)), pltpu.SemaphoreType.REGULAR,
             ],

time: 29.8 us -> 29.3 us (0.983)
  Pallas kernels: 29 us -> 28.5 us
    pallas_call x1, Pallas kernels: 27.1 us -> 26.6 us  [local(): pl.pallas_call(functools.partial(kernel, blocks, parts, chunks), out_shap...]
where the time goes in v6:
time: 29.3 us; the launch traced here: 29.2 us
  Pallas kernels  28.5 us (97%)
  between operations  0.66 us (2%)
    pallas_call x1, Pallas kernels, local(): pl.pallas_call(functools.partial(kernel, blocks, parts, chunks), out_shap...  26.6 us
    pallas_call x1, Pallas kernels, local(): pl.pallas_call(publish, out_shape=(out, out), in_specs=[whole] * 5, out_s...  1.23 us
    pallas_call x1, Pallas kernels, branch(): pl.pallas_call(spread, out_shape=pltpu.VMEM((1, 128), F32), in_specs=[pl....  0.65 us

profile of v6, /device:TPU:0, one launch (start us, length us, event | category | flops | bytes accessed | tf_op | source)
XLA Modules:
  0.0 29.2 jit_solution(9305696720328886602)
XLA Ops:
  0.6 0.7 %conditional.1 = (f32[1,128]{1,0:T(1,128)S(1)}) conditional(s32[]{:T(128)} %clamp.3, (f32[]{:T(128)}) %tuple.18, (f32[]{:T(128)}) %tuple.19, (f32[]{:T(128)}) %tuple.20), branch_computations={%region_0.0_spmd, %region_1.0_spmd, %region_2.0_spmd} | conditional | bytes 8 | solution.py:409
  0.7 0.6 %constant_0.1 = f32[1,128]{1,0:T(1,128)S(1)} custom-call(f32[1]{0:T(128)} %bitcast.value_ref), custom_call_target="tpu_custom_call" | custom-call | tf_op jit(solution)/shard_map/cond/branch_0_fun/constant_0/pallas_call | solution.py:399
  1.3 26.6 %shard_map.80 = (f32[576,384]{1,0:T(8,128)S(1)}, f32[576,384]{1,0:T(8,128)S(1)}, f32[2,576,384]{2,1,0:T(8,128)S(1)}, f32[2,384,128]{2,1,0:T(8,128)S(1)}, f32[2,3,1,128]{3,2,1,0:T(1,128)S(1)}) custom-call(bf16[576,384]{1,0:T(8,128)(2,1)} %bitcast.7, bf16[576,384]{1,0:T(8,128)(2,1)} %bitcast.8, f32[1,128]{1,0:T(1,128)S(1)} %get-tuple-element.29.constant_ref), custom_call_target="tpu_custom_call" | custom-call | tf_op jit(solution)/shard_map/pallas_call | solution.py:411
  28.0 1.2 %shard_map.81 = (f32[576,384]{1,0:T(8,128)}, f32[576,384]{1,0:T(8,128)}) custom-call(f32[576,384]{1,0:T(8,128)S(1)} %get-tuple-element.16.early_ref, f32[576,384]{1,0:T(8,128)S(1)} %get-tuple-element.17.unit_ref, f32[2,576,384]{2,1,0:T(8,128)S(1)} %get-tuple-element.18.sums, f32[2,384,128]{2,1,0:T(8,128)S(1)} %get-tuple-element.19.inner, ...), custom_call_target="tpu_custom_call" | custom-call | tf_op jit(solution)/shard_map/pallas_call | solution.py:432

commit v7 on v6

--- a/solution.py
+++ b/solution.py
@@ -35,7 +35,11 @@
     direct = jnp.logical_not(relayed)
     members = 2 * parts
     end, final = chunks - 1, steps - 1
-    half = width // 2
+    lead = max(3 * width // 4 // 16, 1) * 16
+
+    def cut_rows(cut):
+        return pl.ds(lead, width - lead) if cut else pl.ds(0, lead)
+
     beside = lax.rem(part + 1, parts)
     member = parity * parts + part
 
@@ -97,7 +101,7 @@
             device_id={"dp": near}, device_id_type=MESH)
 
     def end_piece(k, side, slot, cut):
-        return raw.at[k, side, slot, end, pl.ds(cut * half, half)]
+        return raw.at[k, side, slot, end, cut_rows(cut)]
 
     def far_end(cut):
         return pltpu.make_async_remote_copy(
@@ -107,7 +111,7 @@
 
     def relay_end(cut):
         return pltpu.make_async_remote_copy(
-            src_ref=relay.at[end, pl.ds(cut * half, half)], dst_ref=end_piece(2, late, parts - 1, cut),
+            src_ref=relay.at[end, cut_rows(cut)], dst_ref=end_piece(2, late, parts - 1, cut),
             send_sem=far_send, recv_sem=far_recv.at[final + cut],
             device_id={"dp": shifted(2 - 4 * late), "mp": beside}, device_id_type=MESH)
 

time: 29.3 us -> 29.2 us (level)
  no operation moved by 1% of the time
where the time goes in v7:
time: 29.2 us; the launch traced here: 29.1 us
  Pallas kernels  28.4 us (97%)
  between operations  0.66 us (2%)
    pallas_call x1, Pallas kernels, local(): pl.pallas_call(functools.partial(kernel, blocks, parts, chunks), out_shap...  26.5 us
    pallas_call x1, Pallas kernels, local(): pl.pallas_call(publish, out_shape=(out, out), in_specs=[whole] * 5, out_s...  1.23 us
    pallas_call x1, Pallas kernels, branch(): pl.pallas_call(spread, out_shape=pltpu.VMEM((1, 128), F32), in_specs=[pl....  0.65 us

profile of v7, /device:TPU:0, one launch (start us, length us, event | category | flops | bytes accessed | tf_op | source)
XLA Modules:
  0.0 29.1 jit_solution(17361858243861092711)
XLA Ops:
  0.6 0.7 %conditional.1 = (f32[1,128]{1,0:T(1,128)S(1)}) conditional(s32[]{:T(128)} %clamp.3, (f32[]{:T(128)}) %tuple.18, (f32[]{:T(128)}) %tuple.19, (f32[]{:T(128)}) %tuple.20), branch_computations={%region_0.0_spmd, %region_1.0_spmd, %region_2.0_spmd} | conditional | bytes 8 | solution.py:413
  0.7 0.6 %constant_0.1 = f32[1,128]{1,0:T(1,128)S(1)} custom-call(f32[1]{0:T(128)} %bitcast.value_ref), custom_call_target="tpu_custom_call" | custom-call | tf_op jit(solution)/shard_map/cond/branch_0_fun/constant_0/pallas_call | solution.py:403
  1.3 26.5 %shard_map.80 = (f32[576,384]{1,0:T(8,128)S(1)}, f32[576,384]{1,0:T(8,128)S(1)}, f32[2,576,384]{2,1,0:T(8,128)S(1)}, f32[2,384,128]{2,1,0:T(8,128)S(1)}, f32[2,3,1,128]{3,2,1,0:T(1,128)S(1)}) custom-call(bf16[576,384]{1,0:T(8,128)(2,1)} %bitcast.7, bf16[576,384]{1,0:T(8,128)(2,1)} %bitcast.8, f32[1,128]{1,0:T(1,128)S(1)} %get-tuple-element.29.constant_ref), custom_call_target="tpu_custom_call" | custom-call | tf_op jit(solution)/shard_map/pallas_call | solution.py:415
  27.9 1.2 %shard_map.81 = (f32[576,384]{1,0:T(8,128)}, f32[576,384]{1,0:T(8,128)}) custom-call(f32[576,384]{1,0:T(8,128)S(1)} %get-tuple-element.16.early_ref, f32[576,384]{1,0:T(8,128)S(1)} %get-tuple-element.17.unit_ref, f32[2,576,384]{2,1,0:T(8,128)S(1)} %get-tuple-element.18.sums, f32[2,384,128]{2,1,0:T(8,128)S(1)} %get-tuple-element.19.inner, ...), custom_call_target="tpu_custom_call" | custom-call | tf_op jit(solution)/shard_map/pallas_call | solution.py:436

commit v8 on v7

--- a/solution.py
+++ b/solution.py
@@ -312,12 +312,12 @@
 
     def arrive_end():
         for cut in (0, 1):
+            near_end(cut).wait_recv()
+            for offset in range(1, parts):
+                share_end(1, cut, offset).start()
             far_end(cut).wait_recv()
             for offset in range(1, parts):
                 share_end(2, cut, offset).start()
-            near_end(cut).wait_recv()
-            for offset in range(1, parts):
-                share_end(1, cut, offset).start()
 
     def advance(step, carry):
         @pl.when(step < final)

time: 29.2 us -> 29.2 us (level)
  no operation moved by 1% of the time
where the time goes in v8:
time: 29.2 us; the launch traced here: 29.1 us
  Pallas kernels  28.4 us (97%)
  between operations  0.66 us (2%)
    pallas_call x1, Pallas kernels, local(): pl.pallas_call(functools.partial(kernel, blocks, parts, chunks), out_shap...  26.5 us
    pallas_call x1, Pallas kernels, local(): pl.pallas_call(publish, out_shape=(out, out), in_specs=[whole] * 5, out_s...  1.23 us
    pallas_call x1, Pallas kernels, branch(): pl.pallas_call(spread, out_shape=pltpu.VMEM((1, 128), F32), in_specs=[pl....  0.65 us

profile of v8, /device:TPU:0, one launch (start us, length us, event | category | flops | bytes accessed | tf_op | source)
XLA Modules:
  0.0 29.1 jit_solution(3714526591719900742)
XLA Ops:
  0.6 0.7 %conditional.1 = (f32[1,128]{1,0:T(1,128)S(1)}) conditional(s32[]{:T(128)} %clamp.3, (f32[]{:T(128)}) %tuple.18, (f32[]{:T(128)}) %tuple.19, (f32[]{:T(128)}) %tuple.20), branch_computations={%region_0.0_spmd, %region_1.0_spmd, %region_2.0_spmd} | conditional | bytes 8 | solution.py:413
  0.7 0.6 %constant_0.1 = f32[1,128]{1,0:T(1,128)S(1)} custom-call(f32[1]{0:T(128)} %bitcast.value_ref), custom_call_target="tpu_custom_call" | custom-call | tf_op jit(solution)/shard_map/cond/branch_0_fun/constant_0/pallas_call | solution.py:403
  1.3 26.5 %shard_map.80 = (f32[576,384]{1,0:T(8,128)S(1)}, f32[576,384]{1,0:T(8,128)S(1)}, f32[2,576,384]{2,1,0:T(8,128)S(1)}, f32[2,384,128]{2,1,0:T(8,128)S(1)}, f32[2,3,1,128]{3,2,1,0:T(1,128)S(1)}) custom-call(bf16[576,384]{1,0:T(8,128)(2,1)} %bitcast.7, bf16[576,384]{1,0:T(8,128)(2,1)} %bitcast.8, f32[1,128]{1,0:T(1,128)S(1)} %get-tuple-element.29.constant_ref), custom_call_target="tpu_custom_call" | custom-call | tf_op jit(solution)/shard_map/pallas_call | solution.py:415
  27.9 1.2 %shard_map.81 = (f32[576,384]{1,0:T(8,128)}, f32[576,384]{1,0:T(8,128)}) custom-call(f32[576,384]{1,0:T(8,128)S(1)} %get-tuple-element.16.early_ref, f32[576,384]{1,0:T(8,128)S(1)} %get-tuple-element.17.unit_ref, f32[2,576,384]{2,1,0:T(8,128)S(1)} %get-tuple-element.18.sums, f32[2,384,128]{2,1,0:T(8,128)S(1)} %get-tuple-element.19.inner, ...), custom_call_target="tpu_custom_call" | custom-call | tf_op jit(solution)/shard_map/pallas_call | solution.py:436
